TPU v7x, 32 devices: a whole 2x2x4 slice. The times are simulated.
32 devices in a mesh: slab: 16 (over z, y, x), energy: 2 (over core).
Axes of the slice: x: 2, y: 2, z: 4, core: 2. Of those that a mesh axis runs over, the one named last changes fastest.
Arguments:
- onsite_energy: float32 [32, 128], P('slab'), may hold values from -0.3 to 0.3
- onsite_mixing: float32 [32, 128, 128], P('slab'), may hold values from -0.15625 to 0.15625
- hop_strength: float32 [32, 128], P('slab'), may hold values from 0.8 to 1.2
- hop_mixing: float32 [32, 128, 128], P('slab'), may hold values from -0.15625 to 0.15625
- energy: float32 [2], P('energy'), parts along dimension 0, may hold values from -0.4 to 0.4
- broadening: float32 [2], P('energy'), parts along dimension 0, may hold values from 0.01 to 0.025
Outputs:
- green_real: float32 [64, 128, 128], P(('energy', 'slab')), parts along dimension 0
- green_imag: float32 [64, 128, 128], P(('energy', 'slab')), parts along dimension 0
There are 2 independent parts, one for each index of `energy`. A program takes and returns all parts, laid end to end along the dimension named above; an argument that names none is the same for every part. Nothing has to cross between parts.
All inputs are finite; a program needn't handle non-finite values.
Results may differ from a plain program's by a relative error of at most 0.0007.
Values sent between devices are 32-bit elements; how exact they have to be, the bound alone decides.
A program may use at most 128 MiB of HBM per device.

v0:
```python
import functools

import jax
import jax.numpy as jnp
from jax import lax
from jax.experimental import pallas as pl
from jax.experimental.pallas import tpu as pltpu
from jax.sharding import PartitionSpec as P

TILE = 8


def dot(first, second, precision=lax.Precision.HIGHEST):
    return jnp.dot(first, second, precision=precision, preferred_element_type=jnp.float32)


def product(first, second, precision=lax.Precision.HIGHEST):
    columns = second[0].shape[1]
    left = jnp.concatenate([first[0], first[1]], axis=1)
    right = jnp.concatenate(
        [
            jnp.concatenate([second[0], second[1]], axis=1),
            jnp.concatenate([-second[1], second[0]], axis=1),
        ],
        axis=0,
    )
    out = dot(left, right, precision)
    return (out[:, :columns], out[:, columns:])


def flipped(block):
    return (block[0].T, block[1].T)


def rows(*blocks):
    return tuple(jnp.concatenate([b[part] for b in blocks], axis=0) for part in (0, 1))


def cols(*blocks):
    return tuple(jnp.concatenate([b[part] for b in blocks], axis=1) for part in (0, 1))


def chosen(flag, first, second):
    return tuple(jnp.where(flag, a, b) for a, b in zip(first, second))


def read(ref, *index):
    return (ref[(*index[:-1], index[-1])], ref[(*index[:-1], index[-1] + 1)])


def write(ref, block, *index):
    ref[(*index[:-1], index[-1])] = block[0]
    ref[(*index[:-1], index[-1] + 1)] = block[1]


def eye(size):
    row = lax.broadcasted_iota(jnp.int32, (size, size), 0)
    column = lax.broadcasted_iota(jnp.int32, (size, size), 1)
    return row == column


def times(first_r, first_i, second_r, second_i):
    return (first_r * second_r - first_i * second_i, first_r * second_i + first_i * second_r)


def reciprocal(value):
    guess = pltpu.reciprocal(value, approx=True)
    guess = guess * (2.0 - value * guess)
    return guess * (2.0 - value * guess)


def inverse(block):
    size = block[0].shape[0]
    lane = lax.broadcasted_iota(jnp.int32, (TILE, size), 1)
    sub = lax.broadcasted_iota(jnp.int32, (TILE, size), 0)
    keep = lax.broadcasted_iota(jnp.int32, (size - TILE, size), 1) >= TILE

    def spread(column):
        return jnp.broadcast_to(column, (TILE, size))

    def trip(_, carried):
        real, imag = carried
        top_r, top_i = real[:TILE], imag[:TILE]
        columns = [
            (spread(top_r[:, j : j + 1]), spread(top_i[:, j : j + 1])) for j in range(TILE)
        ]
        for k in range(TILE):
            col_r, col_i = columns[k]
            pivot_r, pivot_i = col_r[k : k + 1], col_i[k : k + 1]
            scale = reciprocal(pivot_r * pivot_r + pivot_i * pivot_i)
            q_r, q_i = pivot_r * scale, -pivot_i * scale
            at = sub == k
            col_r, col_i = jnp.where(at, -1.0, col_r), jnp.where(at, 0.0, col_i)
            for j in range(k + 1, TILE):
                old_r, old_i = columns[j]
                t_r, t_i = times(old_r[k : k + 1], old_i[k : k + 1], q_r, q_i)
                u_r, u_i = times(col_r, col_i, t_r, t_i)
                columns[j] = (jnp.where(at, 0.0, old_r) - u_r, jnp.where(at, 0.0, old_i) - u_i)
            row_r, row_i = times(top_r[k : k + 1], top_i[k : k + 1], q_r, q_i)
            here = lane[:1] == k
            row_r, row_i = jnp.where(here, q_r, row_r), jnp.where(here, q_i, row_i)
            u_r, u_i = times(col_r, col_i, row_r, row_i)
            gone = at | (lane == k)
            top_r = jnp.where(gone, 0.0, top_r) - u_r
            top_i = jnp.where(gone, 0.0, top_i) - u_i
        old_r, old_i = real[TILE:], imag[TILE:]
        new_r, new_i = jnp.where(keep, old_r, 0.0), jnp.where(keep, old_i, 0.0)
        for k in range(TILE):
            u_r, u_i = times(
                old_r[:, k : k + 1], old_i[:, k : k + 1], top_r[k : k + 1], top_i[k : k + 1]
            )
            new_r, new_i = new_r - u_r, new_i - u_i
        real = jnp.concatenate([new_r, top_r], axis=0)
        imag = jnp.concatenate([new_i, top_i], axis=0)
        return pltpu.roll(real, size - TILE, 1), pltpu.roll(imag, size - TILE, 1)

    estimate = lax.fori_loop(0, size // TILE, trip, block)
    residue = product(block, estimate)
    one = jnp.where(eye(size), 1.0, 0.0)
    fix = product(estimate, (one - residue[0], -residue[1]), lax.Precision.DEFAULT)
    return (estimate[0] + fix[0], estimate[1] + fix[1])


def wire(count, energy_ref, broad_ref, onsite_ref, mix_ref, hop_ref, hopmix_ref, real_ref, imag_ref,
         crit_out, crit_in, rest_out, rest_in, own_ref, crit_sent, crit_got, rest_sent, rest_got):
    levels = count.bit_length() - 1
    size = mix_ref.shape[1]
    me = lax.axis_index("slab")

    def bit(stride):
        return (me // stride) % 2

    def partner(stride):
        return me + stride - 2 * stride * bit(stride)

    def copies(level, stride):
        target = {"slab": partner(stride)}
        return tuple(
            pltpu.make_async_remote_copy(
                src_ref=out.at[level], dst_ref=into.at[level], send_sem=sent.at[level],
                recv_sem=got.at[level], device_id=target,
                device_id_type=pl.DeviceIdType.MESH,
            )
            for out, into, sent, got in (
                (crit_out, crit_in, crit_sent, crit_got),
                (rest_out, rest_in, rest_sent, rest_got),
            )
        )

    barrier = pltpu.get_barrier_semaphore()
    for level in range(levels):
        pl.semaphore_signal(
            barrier, inc=1, device_id={"slab": partner(1 << level)},
            device_id_type=pl.DeviceIdType.MESH,
        )

    unit = eye(size)
    diagonal_i = jnp.where(unit, broad_ref[0], 0.0)

    def onsite(k):
        mixing = mix_ref[k]
        diagonal = jnp.where(unit, energy_ref[0] - onsite_ref[k : k + 1, :], 0.0)
        return diagonal - 0.5 * (mixing + mixing.T)

    def coupling(k):
        return jnp.where(unit, hop_ref[k : k + 1, :], 0.0) + hopmix_ref[k]

    middle = inverse((onsite(1), diagonal_i))
    lower = coupling(0)
    upper = jnp.where(me == count - 1, 0.0, coupling(1))
    weighted = dot(
        jnp.concatenate([middle[0], middle[1]], axis=0),
        jnp.concatenate([lower.T, upper], axis=1),
    )
    to_low = (weighted[:size, :size], weighted[size:, :size])
    to_high = (weighted[:size, size:], weighted[size:, size:])
    outs = dot(
        jnp.concatenate([lower, upper.T], axis=0),
        jnp.concatenate([to_low[0], to_low[1], to_high[0], to_high[1]], axis=1),
    )
    alpha = (onsite(0) - outs[:size, :size], diagonal_i - outs[:size, size : 2 * size])
    link = (outs[:size, 2 * size : 3 * size], outs[:size, 3 * size :])
    beta = (outs[size:, 2 * size : 3 * size], outs[size:, 3 * size :])
    high = bit(1) > 0
    write(crit_out, chosen(high, alpha, beta), 0, 0)
    write(rest_out, link, 0, 0)
    write(rest_out, chosen(high, beta, alpha), 0, 2)
    zero = jnp.zeros((size, size), jnp.float32)
    one = jnp.where(unit, 1.0, 0.0)
    write(own_ref, (zero, zero), 0, 0)
    write(own_ref, (one, zero), 0, 2)
    write(own_ref, (zero, zero), 0, 4)
    write(own_ref, middle, 1, 0)
    write(own_ref, to_low, 1, 2)
    write(own_ref, to_high, 1, 4)
    pl.semaphore_wait(barrier, levels)
    for copy in copies(0, 1):
        copy.start()

    def eliminated(level, high):
        sign = jnp.where(high, 1.0, -1.0)
        mine, other = read(crit_out, level, 0), read(crit_in, level, 0)
        return inverse((sign * (mine[0] - other[0]), sign * (mine[1] - other[1])))

    def links(level, high):
        mine, other = read(rest_out, level, 0), read(rest_in, level, 0)
        return chosen(high, other, mine), chosen(high, mine, other)

    def ends(level, high):
        mine, other = read(rest_out, level, 2), read(rest_in, level, 2)
        return chosen(high, other, mine), chosen(high, mine, other)

    def step(level, stride):
        high = bit(stride) > 0
        crit, rest = copies(level, stride)
        crit.wait_recv()
        y = eliminated(level, high)
        rest.wait_recv()
        low_link, high_link = links(level, high)
        alpha, beta = ends(level, high)
        legs = cols(flipped(low_link), high_link)
        weighted = product(rows(low_link, flipped(high_link)), y)
        outs = product(weighted, legs)
        alpha = tuple(a - o[:size, :size] for a, o in zip(alpha, outs))
        link = tuple(o[:size, size:] for o in outs)
        beta = tuple(b + o[size:, size:] for b, o in zip(beta, outs))
        following = bit(2 * stride) > 0
        write(crit_out, chosen(following, alpha, beta), level + 1, 0)
        write(rest_out, link, level + 1, 0)
        write(rest_out, chosen(following, beta, alpha), level + 1, 2)
        for copy in copies(level + 1, 2 * stride):
            copy.start()
        states = [[read(own_ref, k, 2 * piece) for piece in range(3)] for k in range(2)]
        used = [chosen(high, state[1], state[2]) for state in states]
        weighted = product(rows(*used), y)
        moved = product(weighted, legs)
        for k, state in enumerate(states):
            part = slice(k * size, (k + 1) * size)
            own = product((weighted[0][part], weighted[1][part]), flipped(used[k]))
            write(own_ref, tuple(s + o for s, o in zip(state[0], own)), k, 0)
            down = tuple(
                jnp.where(high, 0.0, s) + m[part, :size] for s, m in zip(state[1], moved)
            )
            up = tuple(
                jnp.where(high, s, 0.0) + m[part, size:] for s, m in zip(state[2], moved)
            )
            write(own_ref, down, k, 2)
            write(own_ref, up, k, 4)
        return 2 * stride

    stride = lax.fori_loop(0, levels - 1, step, jnp.int32(1))
    last = levels - 1
    high = bit(stride) > 0
    crit, rest = copies(last, stride)
    crit.wait_recv()
    y = eliminated(last, high)
    rest.wait_recv()
    low_link, _ = links(last, high)
    alpha, _ = ends(last, high)
    across = flipped(low_link)
    outs = product(product(low_link, y), across)
    top = inverse((alpha[0] - outs[0], alpha[1] - outs[1]))
    states = [[read(own_ref, k, 2 * piece) for piece in range(3)] for k in range(2)]
    used = [chosen(high, state[1], state[2]) for state in states]
    weighted = product(rows(*used), y)
    moved = product(weighted, across)
    legs = [
        tuple(
            jnp.where(high, 0.0, s) + m[k * size : (k + 1) * size] for s, m in zip(states[k][1], moved)
        )
        for k in range(2)
    ]
    carried = product(rows(*legs), top)
    for k in range(2):
        part = slice(k * size, (k + 1) * size)
        own = product(
            cols((weighted[0][part], weighted[1][part]), (carried[0][part], carried[1][part])),
            rows(flipped(used[k]), flipped(legs[k])),
        )
        real_ref[k] = states[k][0][0] + own[0]
        imag_ref[k] = states[k][0][1] + own[1]

    def drain(level, stride):
        for copy in copies(level, stride):
            copy.wait_send()
        return 2 * stride

    lax.fori_loop(0, levels, drain, jnp.int32(1))


def shards(onsite_energy, onsite_mixing, hop_strength, hop_mixing, energy, broadening):
    size = onsite_mixing.shape[1]
    count = lax.axis_size("slab")
    levels = count.bit_length() - 1
    vmem = pl.BlockSpec(memory_space=pltpu.VMEM)
    smem = pl.BlockSpec(memory_space=pltpu.SMEM)
    out = jax.ShapeDtypeStruct(onsite_mixing.shape, jnp.float32)
    crit = pltpu.VMEM((levels, 2, size, size), jnp.float32)
    rest = pltpu.VMEM((levels, 4, size, size), jnp.float32)
    return pl.pallas_call(
        functools.partial(wire, count),
        out_shape=[out, out],
        in_specs=[smem] * 2 + [vmem] * 4,
        out_specs=[vmem, vmem],
        scratch_shapes=[crit, crit, rest, rest, pltpu.VMEM((2, 6, size, size), jnp.float32)]
        + [pltpu.SemaphoreType.DMA((levels,))] * 4,
        compiler_params=pltpu.CompilerParams(collective_id=0, has_side_effects=True),
        name="wire",
    )(energy, broadening, onsite_energy, onsite_mixing, hop_strength, hop_mixing)


def solution(mesh):
    return jax.shard_map(
        shards,
        mesh=mesh,
        in_specs=(
            P("slab", None),
            P("slab", None, None),
            P("slab", None),
            P("slab", None, None),
            P("energy"),
            P("energy"),
        ),
        out_specs=(P(("energy", "slab"), None, None), P(("energy", "slab"), None, None)),
        check_vma=False,
    )
```

profile of v0, /device:TPU:0, one launch (start us, length us, event | category | flops | bytes accessed | tf_op | source)
XLA Modules:
  0.0 94.9 jit_solution(12596507618266372982)
XLA Ops:
  1.9 90.7 %wire.1 = (f32[2,128,128]{2,1,0:T(8,128)}, f32[2,128,128]{2,1,0:T(8,128)}) custom-call(f32[1]{0:T(128)S(6)} %copy.10.energy_ref, f32[1]{0:T(128)S(6)} %copy.11.broad_ref, f32[2,128]{1,0:T(2,128)} %onsite_ref.1, f32[2,128,128]{2,1,0:T(8,128)} %mix_ref.1, f32[2,128]{1,0:T(2,128)} %hop_ref.1, f32[2,128,128]{2,1,0:T(8,128)} %hopmix_ref.1), custom_call_target="tpu_custom_call" | custom-call | tf_op jit(solution)/shard_map/wire/pallas_call | solution.py:300
  92.7 0.0 copy-start
  92.7 1.6 %copy.12 = f32[2,128,128]{2,1,0:T(8,128)} copy(f32[2,128,128]{2,1,0:T(8,128)} %get-tuple-element.4) | data formatting | bytes 262144
  94.3 0.0 copy-done
  94.3 0.7 copy.13
Async XLA Ops:
  92.7 1.6 %copy-start = (f32[2,128,128]{2,1,0:T(8,128)S(1)}, f32[2,128,128]{2,1,0:T(8,128)}, u32[]{:S(2)}) copy-start(f32[2,128,128]{2,1,0:T(8,128)} %get-tuple-element.5) | copy-start | bytes 393220
where the time goes:
time: 95.1 us; the launch traced here: 94.9 us
  Pallas kernels  90.7 us (95%)
  local copies, waits for them, and re-layouts  2.26 us (2%)
  between operations  1.94 us (2%)
    pallas_call x1, Pallas kernels, shards(): pl.pallas_call(functools.partial(wire, count), out_shape=[out, out], in_s...  90.7 us
    unnamed x4, local copies, waits for them, and re-layouts  2.26 us

commit v1 on v0

v1 whole, which is shorter than its diff:
```python
import functools

import jax
import jax.numpy as jnp
from jax import lax
from jax.experimental import pallas as pl
from jax.experimental.pallas import tpu as pltpu
from jax.sharding import PartitionSpec as P

TILE = 8


def dot(first, second, precision=lax.Precision.HIGHEST):
    return jnp.dot(first, second, precision=precision, preferred_element_type=jnp.float32)


def product(first, second, precision=lax.Precision.HIGHEST):
    columns = second[0].shape[1]
    left = jnp.concatenate([first[0], first[1]], axis=1)
    right = jnp.concatenate(
        [
            jnp.concatenate([second[0], second[1]], axis=1),
            jnp.concatenate([-second[1], second[0]], axis=1),
        ],
        axis=0,
    )
    out = dot(left, right, precision)
    return (out[:, :columns], out[:, columns:])


def flipped(block):
    return (block[0].T, block[1].T)


def rows(*blocks):
    return tuple(jnp.concatenate([b[part] for b in blocks], axis=0) for part in (0, 1))


def cols(*blocks):
    return tuple(jnp.concatenate([b[part] for b in blocks], axis=1) for part in (0, 1))


def chosen(flag, first, second):
    return tuple(jnp.where(flag, a, b) for a, b in zip(first, second))


def read(ref, *index):
    return (ref[(*index[:-1], index[-1])], ref[(*index[:-1], index[-1] + 1)])


def write(ref, block, *index):
    ref[(*index[:-1], index[-1])] = block[0]
    ref[(*index[:-1], index[-1] + 1)] = block[1]


def eye(size):
    row = lax.broadcasted_iota(jnp.int32, (size, size), 0)
    column = lax.broadcasted_iota(jnp.int32, (size, size), 1)
    return row == column


def times(a, b):
    return (a[0] * b[0] - a[1] * b[1], a[0] * b[1] + a[1] * b[0])

def plus(a, b):
    return (a[0] + b[0], a[1] + b[1])

def minus(a, b):
    return (a[0] - b[0], a[1] - b[1])

def total(terms):
    while len(terms) > 1:
        terms = [plus(*terms[i : i + 2]) if i + 1 < len(terms) else terms[i] for i in range(0, len(terms), 2)]
    return terms[0]

def pick(flag, value, block):
    return (jnp.where(flag, value, block[0]), jnp.where(flag, 0.0, block[1]))

def sweep(rows, tile, panel, lane, sub):
    size = lane.shape[1]
    first = TILE * tile
    def column(block, j):
        at = first + j
        index = jnp.full((TILE, size), at, jnp.int32)
        return tuple(jnp.take_along_axis(b, index, axis=1) for b in block)
    def row(block, j):
        return tuple(jnp.broadcast_to(b[j : j + 1], (TILE, size)) for b in block)
    own = rows[tile]
    columns = [column(own, j) for j in range(TILE)]
    others = [v for v in panel if v != tile]
    if tile + 1 in others:
        others.remove(tile + 1); others.insert(0, tile + 1)
    sides = {v: [column(rows[v], j) for j in range(TILE)] for v in others}
    inside = (lane >= first) & (lane < first + TILE)
    unit = jnp.where(lane - first == sub, 1.0, 0.0)
    own = pick(inside, unit, own)
    for p in range(0, TILE, 2):
        low, high = columns[p], columns[p + 1]
        a, b, d = row(low, p), row(high, p), row(high, p + 1)
        det = minus(times(a, d), times(b, b))
        scale = 1.0 / (det[0] * det[0] + det[1] * det[1])
        q = (det[0] * scale, -det[1] * scale)
        at_low, at_high = sub == p, sub == p + 1
        here = at_low | at_high
        low = pick(at_high, 0.0, pick(at_low, -1.0, low))
        high = pick(at_low, 0.0, pick(at_high, -1.0, high))
        e_low = minus(times(low, d), times(high, b))
        e_high = minus(times(high, a), times(low, b))
        d_low, d_high = times(e_low, q), times(e_high, q)
        for j in range(p + 2, TILE):
            old = columns[j]
            up, down = row(old, p), row(old, p + 1)
            kept = pick(here, 0.0, old)
            if j < p + 4:
                change = times(plus(times(e_low, up), times(e_high, down)), q)
            else:
                change = plus(times(d_low, up), times(d_high, down))
            columns[j] = minus(kept, change)
        up, down = row(own, p), row(own, p + 1)
        own = minus(pick(here, 0.0, own), plus(times(d_low, up), times(d_high, down)))
    rows[tile] = own
    spread = [row(own, j) for j in range(TILE)]
    for v in others:
        change = total([times(sides[v][j], spread[j]) for j in range(TILE)])
        rows[v] = minus(pick(inside, 0.0, rows[v]), change)

def inverse(block, parts=4, ahead=2):
    size = block[0].shape[0]
    lane = lax.broadcasted_iota(jnp.int32, (TILE, size), 1)
    sub = lax.broadcasted_iota(jnp.int32, (TILE, size), 0)
    count = size // TILE
    rows = [tuple(b[TILE * v : TILE * v + TILE] for b in block) for v in range(count)]
    step = count // parts
    def stack(which):
        return tuple(jnp.concatenate([rows[v][c] for v in which], axis=0) for c in (0, 1))
    for h in range(parts):
        panel = list(range(h * step, h * step + step))
        ready = [v for v in range(panel[-1] + 1, min(panel[-1] + 1 + ahead, count))]
        rest = [v for v in range(count) if v not in panel + ready]
        start = {v: rows[v] for v in rest}
        for tile in panel:
            sweep(rows, tile, panel + ready, lane, sub)
        if not rest:
            break
        real, imag = stack(panel)
        def pad(x):
            out = []
            if h: out.append(jnp.zeros((h * step * TILE, size), jnp.float32))
            out.append(x)
            if h + 1 < parts: out.append(jnp.zeros(((parts - 1 - h) * step * TILE, size), jnp.float32))
            return jnp.concatenate(out, axis=0)
        right = jnp.concatenate([jnp.concatenate([pad(real), pad(imag)], axis=1), jnp.concatenate([pad(-imag), pad(real)], axis=1)], axis=0)
        left = jnp.concatenate(list(stack(rest)), axis=1)
        out = dot(left, right)
        gone = (lane >= h * step * TILE) & (lane < (h + 1) * step * TILE)
        for n, v in enumerate(rest):
            part = out[TILE * n : TILE * n + TILE]
            rows[v] = minus(pick(gone, 0.0, rows[v]), (part[:, :size], part[:, size:]))
    return stack(range(count))


def pack(block, row, column):
    diagonal = jnp.sum(jnp.where(row == column, block[1], 0.0), axis=0, keepdims=True)
    return jnp.concatenate(
        [jnp.where(row <= column, block[0], block[1]), jnp.broadcast_to(diagonal, (TILE, block[0].shape[1]))],
        axis=0,
    )


def unpack(packed, row, column):
    size = packed.shape[1]
    block = packed[:size]
    mirror = block.T
    diagonal = packed[size : size + 1]
    return (
        jnp.where(row <= column, block, mirror),
        jnp.where(row == column, diagonal, jnp.where(row > column, block, mirror)),
    )


def wire(count, energy_ref, broad_ref, onsite_ref, mix_ref, hop_ref, hopmix_ref, real_ref, imag_ref,
         crit_out, crit_in, rest_out, rest_in, own_ref, crit_sent, crit_got, rest_sent, rest_got):
    levels = count.bit_length() - 1
    last = levels - 1
    size = mix_ref.shape[1]
    me = lax.axis_index("slab")
    row = lax.broadcasted_iota(jnp.int32, (size, size), 0)
    column = lax.broadcasted_iota(jnp.int32, (size, size), 1)

    def bit(stride):
        return (me // stride) % 2

    def partner(stride):
        return me + stride - 2 * stride * bit(stride)

    def copy(level, stride, out, into, sent, got):
        return pltpu.make_async_remote_copy(
            src_ref=out.at[level], dst_ref=into.at[level], send_sem=sent.at[level],
            recv_sem=got.at[level], device_id={"slab": partner(stride)},
            device_id_type=pl.DeviceIdType.MESH,
        )

    def crit(level, stride):
        return copy(level, stride, crit_out, crit_in, crit_sent, crit_got)

    def rest(level, stride):
        return copy(level, stride, rest_out, rest_in, rest_sent, rest_got)

    def write_rest(level, link, end):
        rest_out[level, :size] = link[0]
        rest_out[level, size : 2 * size] = link[1]
        rest_out[level, 2 * size :] = end

    def link_of(ref, level):
        return (ref[level, :size], ref[level, size : 2 * size])

    barrier = pltpu.get_barrier_semaphore()
    for level in range(levels):
        pl.semaphore_signal(
            barrier, inc=1, device_id={"slab": partner(1 << level)},
            device_id_type=pl.DeviceIdType.MESH,
        )

    unit = row == column
    diagonal_i = jnp.where(unit, broad_ref[0], 0.0)

    def onsite(k):
        mixing = mix_ref[k]
        diagonal = jnp.where(unit, energy_ref[0] - onsite_ref[k : k + 1, :], 0.0)
        return diagonal - 0.5 * (mixing + mixing.T)

    def coupling(k):
        return jnp.where(unit, hop_ref[k : k + 1, :], 0.0) + hopmix_ref[k]

    def halves(out):
        return (out[:, :size], out[:, size:])

    middle = inverse((onsite(1), diagonal_i))
    lower = coupling(0)
    upper = jnp.where(me == count - 1, 0.0, coupling(1))
    lower_t, upper_t = lower.T, upper.T
    high = bit(1) > 0
    both = jnp.concatenate([middle[0], middle[1]], axis=0)
    first = jnp.where(high, lower_t, upper)
    weighted = dot(both, first)
    near = (weighted[:size], weighted[size:])
    outs = halves(dot(jnp.where(high, lower, upper_t), jnp.concatenate(near, axis=1)))
    alpha = pack((onsite(0), diagonal_i), row, column)
    change = pack(outs, row, column)
    crit_out[0] = jnp.where(high, alpha - change, change)
    pl.semaphore_wait(barrier, levels)
    if levels > 1:
        crit(0, 1).start()
    weighted = dot(both, jnp.where(high, upper, lower_t))
    far = (weighted[:size], weighted[size:])
    to_low, to_high = chosen(high, near, far), chosen(high, far, near)
    outs = halves(dot(jnp.where(high, upper_t, lower), jnp.concatenate(far, axis=1)))
    link = halves(dot(lower, jnp.concatenate(to_high, axis=1)))
    change = pack(outs, row, column)
    write_rest(0, link, jnp.where(high, change, alpha - change))
    if levels > 1:
        rest(0, 1).start()
    zero = jnp.zeros((size, size), jnp.float32)
    one = jnp.where(unit, 1.0, 0.0)
    write(own_ref, (zero, zero), 0, 0)
    write(own_ref, (one, zero), 0, 2)
    write(own_ref, (zero, zero), 0, 4)
    write(own_ref, middle, 1, 0)
    write(own_ref, to_low, 1, 2)
    write(own_ref, to_high, 1, 4)

    def eliminated(level, high):
        packed = jnp.where(high, 1.0, -1.0) * (crit_out[level] - crit_in[level])
        return inverse(unpack(packed, row, column))

    def step(level, stride):
        high = bit(stride) > 0
        crit(level, stride).wait_recv()
        y = eliminated(level, high)
        rest(level, stride).wait_recv()
        mine, other = link_of(rest_out, level), link_of(rest_in, level)
        low_link, high_link = chosen(high, other, mine), chosen(high, mine, other)
        mine, other = rest_out[level, 2 * size :], rest_in[level, 2 * size :]
        alpha, beta = jnp.where(high, other, mine), jnp.where(high, mine, other)
        low_t, high_t = flipped(low_link), flipped(high_link)
        following = bit(2 * stride) > 0
        near = product(chosen(following, low_link, high_t), y)
        change = pack(product(near, chosen(following, low_t, high_link)), row, column)
        crit_out[level + 1] = jnp.where(following, alpha - change, beta + change)

        @pl.when(level + 1 < last)
        def _():
            crit(level + 1, 2 * stride).start()

        far = product(chosen(following, high_t, low_link), y)
        change = pack(product(far, chosen(following, high_link, low_t)), row, column)
        link = product(chosen(following, near, far), high_link)
        write_rest(level + 1, link, jnp.where(following, beta + change, alpha - change))

        @pl.when(level + 1 < last)
        def _():
            rest(level + 1, 2 * stride).start()

        legs = cols(low_t, high_link)
        states = [[read(own_ref, k, 2 * piece) for piece in range(3)] for k in range(2)]
        used = [chosen(high, state[1], state[2]) for state in states]
        weighted = product(rows(*used), y)
        moved = product(weighted, legs)
        for k, state in enumerate(states):
            part = slice(k * size, (k + 1) * size)
            own = product((weighted[0][part], weighted[1][part]), flipped(used[k]))
            write(own_ref, tuple(s + o for s, o in zip(state[0], own)), k, 0)
            down = tuple(
                jnp.where(high, 0.0, s) + m[part, :size] for s, m in zip(state[1], moved)
            )
            up = tuple(
                jnp.where(high, s, 0.0) + m[part, size:] for s, m in zip(state[2], moved)
            )
            write(own_ref, down, k, 2)
            write(own_ref, up, k, 4)
        return 2 * stride

    stride = lax.fori_loop(0, last, step, jnp.int32(1))
    high = bit(stride) > 0
    mine, end = crit_out[last], rest_out[last, 2 * size :]
    link = link_of(rest_out, last)
    ground = inverse(unpack(jnp.where(high, mine, end), row, column))
    change = pack(product(product(flipped(link), ground), link), row, column)
    crit_out[last] = jnp.where(high, mine, mine + change)
    crit(last, stride).start()
    states = [[read(own_ref, k, 2 * piece) for piece in range(3)] for k in range(2)]
    weighted = product(rows(*(state[1] for state in states)), ground)
    moved = product(weighted, link)
    owns, legs = [], []
    for k, state in enumerate(states):
        part = slice(k * size, (k + 1) * size)
        own = product((weighted[0][part], weighted[1][part]), flipped(state[1]))
        owns.append(tuple(s + jnp.where(high, 0.0, o) for s, o in zip(state[0], own)))
        legs.append(
            tuple(jnp.where(high, d, u + m[part]) for d, u, m in zip(state[1], state[2], moved))
        )
    crit(last, stride).wait_recv()
    y = eliminated(last, high)
    weighted = product(rows(*legs), y)
    for k in range(2):
        part = slice(k * size, (k + 1) * size)
        out = product((weighted[0][part], weighted[1][part]), flipped(legs[k]))
        real_ref[k] = owns[k][0] + out[0]
        imag_ref[k] = owns[k][1] + out[1]

    def drain(level, stride):
        crit(level, stride).wait_send()
        rest(level, stride).wait_send()
        return 2 * stride

    stride = lax.fori_loop(0, last, drain, jnp.int32(1))
    crit(last, stride).wait_send()


def shards(onsite_energy, onsite_mixing, hop_strength, hop_mixing, energy, broadening):
    size = onsite_mixing.shape[1]
    count = lax.axis_size("slab")
    levels = count.bit_length() - 1
    vmem = pl.BlockSpec(memory_space=pltpu.VMEM)
    smem = pl.BlockSpec(memory_space=pltpu.SMEM)
    out = jax.ShapeDtypeStruct(onsite_mixing.shape, jnp.float32)
    crit = pltpu.VMEM((levels, size + TILE, size), jnp.float32)
    rest = pltpu.VMEM((levels, 3 * size + TILE, size), jnp.float32)
    return pl.pallas_call(
        functools.partial(wire, count),
        out_shape=[out, out],
        in_specs=[smem] * 2 + [vmem] * 4,
        out_specs=[vmem, vmem],
        scratch_shapes=[crit, crit, rest, rest, pltpu.VMEM((2, 6, size, size), jnp.float32)]
        + [pltpu.SemaphoreType.DMA((levels,))] * 4,
        compiler_params=pltpu.CompilerParams(collective_id=0, has_side_effects=True),
        name="wire",
    )(energy, broadening, onsite_energy, onsite_mixing, hop_strength, hop_mixing)


def solution(mesh):
    return jax.shard_map(
        shards,
        mesh=mesh,
        in_specs=(
            P("slab", None),
            P("slab", None, None),
            P("slab", None),
            P("slab", None, None),
            P("energy"),
            P("energy"),
        ),
        out_specs=(P(("energy", "slab"), None, None), P(("energy", "slab"), None, None)),
        check_vma=False,
    )
```

time: 95.1 us -> 60.9 us (0.64)
  Pallas kernels: 90.7 us -> 56.5 us
    pallas_call x1, Pallas kernels: 90.7 us -> 56.5 us  [shards(): pl.pallas_call(functools.partial(wire, count), out_shape=[out, out], in_s...]
where the time goes in v1:
time: 60.9 us; the launch traced here: 60.7 us
  Pallas kernels  56.5 us (93%)
  local copies, waits for them, and re-layouts  2.26 us (4%)
  between operations  1.94 us (3%)
    pallas_call x1, Pallas kernels, shards(): pl.pallas_call(functools.partial(wire, count), out_shape=[out, out], in_s...  56.5 us
    unnamed x4, local copies, waits for them, and re-layouts  2.26 us

profile of v1, /device:TPU:0, one launch (start us, length us, event | category | flops | bytes accessed | tf_op | source)
XLA Modules:
  0.0 60.7 jit_solution(11890494734809916761)
XLA Ops:
  1.9 56.5 %wire.1 = (f32[2,128,128]{2,1,0:T(8,128)}, f32[2,128,128]{2,1,0:T(8,128)}) custom-call(f32[1]{0:T(128)S(6)} %copy.10.energy_ref, f32[1]{0:T(128)S(6)} %copy.11.broad_ref, f32[2,128]{1,0:T(2,128)} %onsite_ref.1, f32[2,128,128]{2,1,0:T(8,128)} %mix_ref.1, f32[2,128]{1,0:T(2,128)} %hop_ref.1, f32[2,128,128]{2,1,0:T(8,128)} %hopmix_ref.1), custom_call_target="tpu_custom_call" | custom-call | tf_op jit(solution)/shard_map/wire/pallas_call | solution.py:369
  58.5 0.0 copy-start
  58.5 1.6 %copy.12 = f32[2,128,128]{2,1,0:T(8,128)} copy(f32[2,128,128]{2,1,0:T(8,128)} %get-tuple-element.4) | data formatting | bytes 262144
  60.1 0.0 copy-done
  60.1 0.7 %copy.13 = f32[2,128,128]{2,1,0:T(8,128)} copy(f32[2,128,128]{2,1,0:T(8,128)S(1)} %copy-done) | data formatting | bytes 262144
Async XLA Ops:
  58.5 1.6 %copy-start = (f32[2,128,128]{2,1,0:T(8,128)S(1)}, f32[2,128,128]{2,1,0:T(8,128)}, u32[]{:S(2)}) copy-start(f32[2,128,128]{2,1,0:T(8,128)} %get-tuple-element.5) | copy-start | bytes 393220

commit v2 on v1

--- a/solution.py
+++ b/solution.py
@@ -111,10 +111,7 @@
             old = columns[j]
             up, down = row(old, p), row(old, p + 1)
             kept = pick(here, 0.0, old)
-            if j < p + 4:
-                change = times(plus(times(e_low, up), times(e_high, down)), q)
-            else:
-                change = plus(times(d_low, up), times(d_high, down))
+            change = plus(times(d_low, up), times(d_high, down))
             columns[j] = minus(kept, change)
         up, down = row(own, p), row(own, p + 1)
         own = minus(pick(here, 0.0, own), plus(times(d_low, up), times(d_high, down)))
@@ -129,34 +126,32 @@
     lane = lax.broadcasted_iota(jnp.int32, (TILE, size), 1)
     sub = lax.broadcasted_iota(jnp.int32, (TILE, size), 0)
     count = size // TILE
-    rows = [tuple(b[TILE * v : TILE * v + TILE] for b in block) for v in range(count)]
     step = count // parts
-    def stack(which):
-        return tuple(jnp.concatenate([rows[v][c] for v in which], axis=0) for c in (0, 1))
-    for h in range(parts):
-        panel = list(range(h * step, h * step + step))
-        ready = [v for v in range(panel[-1] + 1, min(panel[-1] + 1 + ahead, count))]
-        rest = [v for v in range(count) if v not in panel + ready]
-        start = {v: rows[v] for v in rest}
-        for tile in panel:
-            sweep(rows, tile, panel + ready, lane, sub)
-        if not rest:
-            break
-        real, imag = stack(panel)
-        def pad(x):
-            out = []
-            if h: out.append(jnp.zeros((h * step * TILE, size), jnp.float32))
-            out.append(x)
-            if h + 1 < parts: out.append(jnp.zeros(((parts - 1 - h) * step * TILE, size), jnp.float32))
-            return jnp.concatenate(out, axis=0)
-        right = jnp.concatenate([jnp.concatenate([pad(real), pad(imag)], axis=1), jnp.concatenate([pad(-imag), pad(real)], axis=1)], axis=0)
-        left = jnp.concatenate(list(stack(rest)), axis=1)
+    width = step * TILE
+
+    def trip(_, carried):
+        rows = [tuple(b[TILE * v : TILE * v + TILE] for b in carried) for v in range(count)]
+        ready = list(range(step, step + ahead))
+        rest = list(range(step + ahead, count))
+        left = jnp.concatenate([carried[0][width + ahead * TILE :], carried[1][width + ahead * TILE :]], axis=1)
+        for tile in range(step):
+            sweep(rows, tile, list(range(step)) + ready, lane, sub)
+        empty = jnp.zeros((size - width, 2 * size), jnp.float32)
+        real, imag = (jnp.concatenate([rows[v][c] for v in range(step)], axis=0) for c in (0, 1))
+        right = jnp.concatenate(
+            [jnp.concatenate([real, imag], axis=1), empty, jnp.concatenate([-imag, real], axis=1), empty], axis=0
+        )
         out = dot(left, right)
-        gone = (lane >= h * step * TILE) & (lane < (h + 1) * step * TILE)
+        gone = lane < width
         for n, v in enumerate(rest):
             part = out[TILE * n : TILE * n + TILE]
             rows[v] = minus(pick(gone, 0.0, rows[v]), (part[:, :size], part[:, size:]))
-    return stack(range(count))
+        order = list(range(step, count)) + list(range(step))
+        return tuple(
+            pltpu.roll(jnp.concatenate([rows[v][c] for v in order], axis=0), size - width, 1) for c in (0, 1)
+        )
+
+    return lax.fori_loop(0, parts, trip, block)
 
 
 def pack(block, row, column):

time: 60.9 us -> 59.2 us (0.972)
  Pallas kernels: 56.5 us -> 54.9 us
    pallas_call x1, Pallas kernels: 56.5 us -> 54.9 us  [shards(): pl.pallas_call(functools.partial(wire, count), out_shape=[out, out], in_s...]
where the time goes in v2:
time: 59.2 us; the launch traced here: 59.1 us
  Pallas kernels  54.9 us (93%)
  local copies, waits for them, and re-layouts  2.26 us (4%)
  between operations  1.94 us (3%)
    pallas_call x1, Pallas kernels, shards(): pl.pallas_call(functools.partial(wire, count), out_shape=[out, out], in_s...  54.9 us
    unnamed x4, local copies, waits for them, and re-layouts  2.26 us

profile of v2, /device:TPU:0, one launch (start us, length us, event | category | flops | bytes accessed | tf_op | source)
XLA Modules:
  0.0 59.1 jit_solution(13530616071037472098)
XLA Ops:
  1.9 54.9 %wire.1 = (f32[2,128,128]{2,1,0:T(8,128)}, f32[2,128,128]{2,1,0:T(8,128)}) custom-call(f32[1]{0:T(128)S(6)} %copy.10.energy_ref, f32[1]{0:T(128)S(6)} %copy.11.broad_ref, f32[2,128]{1,0:T(2,128)} %onsite_ref.1, f32[2,128,128]{2,1,0:T(8,128)} %mix_ref.1, f32[2,128]{1,0:T(2,128)} %hop_ref.1, f32[2,128,128]{2,1,0:T(8,128)} %hopmix_ref.1), custom_call_target="tpu_custom_call" | custom-call | tf_op jit(solution)/shard_map/wire/pallas_call | solution.py:364
  56.8 0.0 copy-start
  56.8 1.6 %copy.12 = f32[2,128,128]{2,1,0:T(8,128)} copy(f32[2,128,128]{2,1,0:T(8,128)} %get-tuple-element.4) | data formatting | bytes 262144
  58.4 0.0 copy-done
  58.4 0.7 %copy.13 = f32[2,128,128]{2,1,0:T(8,128)} copy(f32[2,128,128]{2,1,0:T(8,128)S(1)} %copy-done) | data formatting | bytes 262144
Async XLA Ops:
  56.8 1.6 %copy-start = (f32[2,128,128]{2,1,0:T(8,128)S(1)}, f32[2,128,128]{2,1,0:T(8,128)}, u32[]{:S(2)}) copy-start(f32[2,128,128]{2,1,0:T(8,128)} %get-tuple-element.5) | copy-start | bytes 393220

commit v3 on v2

--- a/solution.py
+++ b/solution.py
@@ -174,7 +174,7 @@
 
 
 def wire(count, energy_ref, broad_ref, onsite_ref, mix_ref, hop_ref, hopmix_ref, real_ref, imag_ref,
-         crit_out, crit_in, rest_out, rest_in, own_ref, crit_sent, crit_got, rest_sent, rest_got):
+         crit_out, crit_in, rest_out, rest_in, own_ref, kept_ref, crit_sent, crit_got, rest_sent, rest_got):
     levels = count.bit_length() - 1
     last = levels - 1
     size = mix_ref.shape[1]
@@ -268,34 +268,7 @@
         packed = jnp.where(high, 1.0, -1.0) * (crit_out[level] - crit_in[level])
         return inverse(unpack(packed, row, column))
 
-    def step(level, stride):
-        high = bit(stride) > 0
-        crit(level, stride).wait_recv()
-        y = eliminated(level, high)
-        rest(level, stride).wait_recv()
-        mine, other = link_of(rest_out, level), link_of(rest_in, level)
-        low_link, high_link = chosen(high, other, mine), chosen(high, mine, other)
-        mine, other = rest_out[level, 2 * size :], rest_in[level, 2 * size :]
-        alpha, beta = jnp.where(high, other, mine), jnp.where(high, mine, other)
-        low_t, high_t = flipped(low_link), flipped(high_link)
-        following = bit(2 * stride) > 0
-        near = product(chosen(following, low_link, high_t), y)
-        change = pack(product(near, chosen(following, low_t, high_link)), row, column)
-        crit_out[level + 1] = jnp.where(following, alpha - change, beta + change)
-
-        @pl.when(level + 1 < last)
-        def _():
-            crit(level + 1, 2 * stride).start()
-
-        far = product(chosen(following, high_t, low_link), y)
-        change = pack(product(far, chosen(following, high_link, low_t)), row, column)
-        link = product(chosen(following, near, far), high_link)
-        write_rest(level + 1, link, jnp.where(following, beta + change, alpha - change))
-
-        @pl.when(level + 1 < last)
-        def _():
-            rest(level + 1, 2 * stride).start()
-
+    def advance(high, y, low_t, high_link):
         legs = cols(low_t, high_link)
         states = [[read(own_ref, k, 2 * piece) for piece in range(3)] for k in range(2)]
         used = [chosen(high, state[1], state[2]) for state in states]
@@ -313,6 +286,42 @@
             )
             write(own_ref, down, k, 2)
             write(own_ref, up, k, 4)
+
+    def step(level, stride):
+        high = bit(stride) > 0
+        crit(level, stride).wait_recv()
+        y = eliminated(level, high)
+        rest(level, stride).wait_recv()
+        mine, other = link_of(rest_out, level), link_of(rest_in, level)
+        low_link, high_link = chosen(high, other, mine), chosen(high, mine, other)
+        mine, other = rest_out[level, 2 * size :], rest_in[level, 2 * size :]
+        alpha, beta = jnp.where(high, other, mine), jnp.where(high, mine, other)
+        low_t, high_t = flipped(low_link), flipped(high_link)
+        following = bit(2 * stride) > 0
+        near = product(chosen(following, low_link, high_t), y)
+        change = pack(product(near, chosen(following, low_t, high_link)), row, column)
+        crit_out[level + 1] = jnp.where(following, alpha - change, beta + change)
+
+        @pl.when(level + 1 < last)
+        def _():
+            crit(level + 1, 2 * stride).start()
+
+        far = product(chosen(following, high_t, low_link), y)
+        change = pack(product(far, chosen(following, high_link, low_t)), row, column)
+        link = product(chosen(following, near, far), high_link)
+        write_rest(level + 1, link, jnp.where(following, beta + change, alpha - change))
+
+        @pl.when(level + 1 < last)
+        def _():
+            rest(level + 1, 2 * stride).start()
+
+        kept_ref[0] = y[0]
+        kept_ref[1] = y[1]
+
+        @pl.when(level + 1 < last)
+        def _():
+            advance(high, y, low_t, high_link)
+
         return 2 * stride
 
     stride = lax.fori_loop(0, last, step, jnp.int32(1))
@@ -323,6 +332,11 @@
     change = pack(product(product(flipped(link), ground), link), row, column)
     crit_out[last] = jnp.where(high, mine, mine + change)
     crit(last, stride).start()
+    if last > 0:
+        before = bit(stride // 2) > 0
+        mine, other = link_of(rest_out, last - 1), link_of(rest_in, last - 1)
+        low_link, high_link = chosen(before, other, mine), chosen(before, mine, other)
+        advance(before, (kept_ref[0], kept_ref[1]), flipped(low_link), high_link)
     states = [[read(own_ref, k, 2 * piece) for piece in range(3)] for k in range(2)]
     weighted = product(rows(*(state[1] for state in states)), ground)
     moved = product(weighted, link)
@@ -366,7 +380,7 @@
         out_shape=[out, out],
         in_specs=[smem] * 2 + [vmem] * 4,
         out_specs=[vmem, vmem],
-        scratch_shapes=[crit, crit, rest, rest, pltpu.VMEM((2, 6, size, size), jnp.float32)]
+        scratch_shapes=[crit, crit, rest, rest, pltpu.VMEM((2, 6, size, size), jnp.float32), pltpu.VMEM((2, size, size), jnp.float32)]
         + [pltpu.SemaphoreType.DMA((levels,))] * 4,
         compiler_params=pltpu.CompilerParams(collective_id=0, has_side_effects=True),
         name="wire",

time: 59.2 us -> 57.7 us (0.975)
  Pallas kernels: 54.9 us -> 53.3 us
    pallas_call x1, Pallas kernels: 54.9 us -> 53.3 us  [shards(): pl.pallas_call(functools.partial(wire, count), out_shape=[out, out], in_s...]
where the time goes in v3:
time: 57.7 us; the launch traced here: 57.5 us
  Pallas kernels  53.3 us (92%)
  local copies, waits for them, and re-layouts  2.26 us (4%)
  between operations  1.94 us (3%)
    pallas_call x1, Pallas kernels, shards(): pl.pallas_call(functools.partial(wire, count), out_shape=[out, out], in_s...  53.3 us
    unnamed x4, local copies, waits for them, and re-layouts  2.26 us

profile of v3, /device:TPU:0, one launch (start us, length us, event | category | flops | bytes accessed | tf_op | source)
XLA Modules:
  0.0 57.5 jit_solution(14615786168185459783)
XLA Ops:
  1.9 53.3 %wire.1 = (f32[2,128,128]{2,1,0:T(8,128)}, f32[2,128,128]{2,1,0:T(8,128)}) custom-call(f32[1]{0:T(128)S(6)} %copy.10.energy_ref, f32[1]{0:T(128)S(6)} %copy.11.broad_ref, f32[2,128]{1,0:T(2,128)} %onsite_ref.1, f32[2,128,128]{2,1,0:T(8,128)} %mix_ref.1, f32[2,128]{1,0:T(2,128)} %hop_ref.1, f32[2,128,128]{2,1,0:T(8,128)} %hopmix_ref.1), custom_call_target="tpu_custom_call" | custom-call | tf_op jit(solution)/shard_map/wire/pallas_call | solution.py:378
  55.3 0.0 copy-start
  55.3 1.6 %copy.12 = f32[2,128,128]{2,1,0:T(8,128)} copy(f32[2,128,128]{2,1,0:T(8,128)} %get-tuple-element.4) | data formatting | bytes 262144
  56.9 0.0 copy-done
  56.9 0.7 %copy.13 = f32[2,128,128]{2,1,0:T(8,128)} copy(f32[2,128,128]{2,1,0:T(8,128)S(1)} %copy-done) | data formatting | bytes 262144
Async XLA Ops:
  55.3 1.6 %copy-start = (f32[2,128,128]{2,1,0:T(8,128)S(1)}, f32[2,128,128]{2,1,0:T(8,128)}, u32[]{:S(2)}) copy-start(f32[2,128,128]{2,1,0:T(8,128)} %get-tuple-element.5) | copy-start | bytes 393220

commit v4 on v3

--- a/solution.py
+++ b/solution.py
@@ -151,7 +151,7 @@
             pltpu.roll(jnp.concatenate([rows[v][c] for v in order], axis=0), size - width, 1) for c in (0, 1)
         )
 
-    return lax.fori_loop(0, parts, trip, block)
+    return lax.fori_loop(0, parts // 2, lambda i, c: trip(i, trip(i, c)), block)
 
 
 def pack(block, row, column):
@@ -311,15 +311,12 @@
         link = product(chosen(following, near, far), high_link)
         write_rest(level + 1, link, jnp.where(following, beta + change, alpha - change))
 
+        kept_ref[0] = y[0]
+        kept_ref[1] = y[1]
+
         @pl.when(level + 1 < last)
         def _():
             rest(level + 1, 2 * stride).start()
-
-        kept_ref[0] = y[0]
-        kept_ref[1] = y[1]
-
-        @pl.when(level + 1 < last)
-        def _():
             advance(high, y, low_t, high_link)
 
         return 2 * stride

time: 57.7 us -> 57.5 us (level)
  no operation moved by 1% of the time
where the time goes in v4:
time: 57.5 us; the launch traced here: 57.3 us
  Pallas kernels  53.1 us (92%)
  local copies, waits for them, and re-layouts  2.26 us (4%)
  between operations  1.94 us (3%)
    pallas_call x1, Pallas kernels, shards(): pl.pallas_call(functools.partial(wire, count), out_shape=[out, out], in_s...  53.1 us
    unnamed x4, local copies, waits for them, and re-layouts  2.26 us

profile of v4, /device:TPU:0, one launch (start us, length us, event | category | flops | bytes accessed | tf_op | source)
XLA Modules:
  0.0 57.3 jit_solution(13413478761286010418)
XLA Ops:
  1.9 53.1 %wire.1 = (f32[2,128,128]{2,1,0:T(8,128)}, f32[2,128,128]{2,1,0:T(8,128)}) custom-call(f32[1]{0:T(128)S(6)} %copy.10.energy_ref, f32[1]{0:T(128)S(6)} %copy.11.broad_ref, f32[2,128]{1,0:T(2,128)} %onsite_ref.1, f32[2,128,128]{2,1,0:T(8,128)} %mix_ref.1, f32[2,128]{1,0:T(2,128)} %hop_ref.1, f32[2,128,128]{2,1,0:T(8,128)} %hopmix_ref.1), custom_call_target="tpu_custom_call" | custom-call | tf_op jit(solution)/shard_map/wire/pallas_call | solution.py:375
  55.1 0.0 copy-start
  55.1 1.6 %copy.12 = f32[2,128,128]{2,1,0:T(8,128)} copy(f32[2,128,128]{2,1,0:T(8,128)} %get-tuple-element.4) | data formatting | bytes 262144
  56.7 0.0 copy-done
  56.7 0.7 %copy.13 = f32[2,128,128]{2,1,0:T(8,128)} copy(f32[2,128,128]{2,1,0:T(8,128)S(1)} %copy-done) | data formatting | bytes 262144
Async XLA Ops:
  55.1 1.6 %copy-start = (f32[2,128,128]{2,1,0:T(8,128)S(1)}, f32[2,128,128]{2,1,0:T(8,128)}, u32[]{:S(2)}) copy-start(f32[2,128,128]{2,1,0:T(8,128)} %get-tuple-element.5) | copy-start | bytes 393220
